TPU v7x, 256 devices: a whole 4x4x8 slice. The times are simulated.
256 devices in a mesh: rp: 8 (over x, z_lo), pb: 32 (over z_hi, y, core).
Axes of the slice: x: 4, y: 4, z: 8 (z_hi: 4, z_lo: 2; z = z_hi * 2 + z_lo), core: 2. Of those that a mesh axis runs over, the one named last changes fastest.
Arguments:
- wannier_g: bfloat16 [2, 1024, 32, 1152], P(None, 'rp', 'pb'), may hold values from -0.19921875 to 0.19921875
- rp_coords: int32 [3, 1024], replicated, may hold values from -8 to 8
- q_coords: int32 [3, 512], P(None, ('rp', 'pb')), may hold values from 0 to 15
- k_index: int32 [1], replicated, may hold values from 0 to 7
- k_vectors: bfloat16 [8, 2, 32, 32], replicated, may hold values from -0.75 to 0.75
- kq_vectors: bfloat16 [512, 2, 32, 32], P(('rp', 'pb')), may hold values from -0.75 to 0.75
- modes: bfloat16 [512, 2, 36, 36], P(('rp', 'pb')), may hold values from -0.75 to 0.75
Outputs:
- rotated: float32 [512, 2, 32, 1152], P(('rp', 'pb'))
All inputs are finite; a program needn't handle non-finite values.
Results may differ from a plain program's by a relative error of at most 0.0054.
Values may be sent and summed in bfloat16 or wider, within the bound.
A program may use at most 64 MiB of HBM per device.

v0:
```python
import math
import jax
import jax.numpy as jnp
from jax import lax
from jax.sharding import PartitionSpec as P

NK = 16


def in_blocks(x, dim, length):
    shape = x.shape
    parts = x.reshape(*shape[:dim], length, shape[dim] // length, *shape[dim + 1 :])
    return jnp.moveaxis(parts, dim, 0)


def joined_along(parts, dim):
    shape = list(parts.shape[1:])
    shape[dim] *= parts.shape[0]
    return jnp.moveaxis(parts, 0, dim).reshape(shape)


def one_exchange(x, axis, axes, splits, concats):
    sizes = [lax.axis_size(a) for a in axes]
    parts = in_blocks(x, splits[0], sizes[0])
    parts = jnp.moveaxis(in_blocks(parts, splits[1] + 1, sizes[1]), 0, 1)
    inside = parts.shape[2:]
    parts = parts.reshape(-1, *inside)
    parts = lax.all_to_all(parts, axis, split_axis=0, concat_axis=0, tiled=True)
    parts = joined_along(parts.reshape(*sizes, *inside), concats[0] + 1)
    return joined_along(parts, concats[1])


def phases(q_rows, r_coords):
    turns = jnp.mod(jnp.sum(q_rows[:, :, None] * r_coords[:, None, :], axis=0), NK)
    angle = turns.astype(jnp.float32) * (2.0 * math.pi / NK)
    cosine = jnp.cos(angle).astype(jnp.bfloat16)
    sine = jnp.sin(angle).astype(jnp.bfloat16)
    return (jnp.concatenate([cosine, -sine], axis=1), jnp.concatenate([sine, cosine], axis=1))


def rotate(fourier, mode_vecs, unit, kq_vecs):
    count = fourier.shape[0]
    bands = kq_vecs.shape[2]
    branches = mode_vecs.shape[2]
    field = fourier.reshape(count, 2, bands, bands, branches)
    e_real, e_imag = (mode_vecs[:, 0], mode_vecs[:, 1])
    e_block = jnp.stack([jnp.stack([e_real, e_imag], 2), jnp.stack([-e_imag, e_real], 2)], 1)
    by_mode = jnp.einsum(
        "qcmnv,qcvdu->qdmnu", field, e_block, preferred_element_type=jnp.float32
    ).astype(jnp.bfloat16)
    u_real, u_imag = (unit[0], unit[1])
    u_block = jnp.stack([jnp.stack([u_real, u_imag], 1), jnp.stack([-u_imag, u_real], 1)], 0)
    by_band = jnp.einsum(
        "qcmnu,cndj->qdmju", by_mode, u_block, preferred_element_type=jnp.float32
    ).astype(jnp.bfloat16)
    v_real, v_imag = (kq_vecs[:, 0], kq_vecs[:, 1])
    v_block = jnp.stack([jnp.stack([v_real, -v_imag], 2), jnp.stack([v_imag, v_real], 2)], 1)
    result = jnp.einsum("qcmju,qcmdi->qdiju", by_band, v_block, preferred_element_type=jnp.float32)
    return result.reshape(count, 2, bands, bands * branches)


def local(wannier_g, rp_coords, q_coords, k_index, k_vectors, kq_vectors, modes):
    q_all = lax.all_gather(q_coords, ("rp", "pb"), axis=1, tiled=True)
    total = q_all.shape[1]
    groups = lax.axis_size("rp")
    block = total // groups
    moved = lax.all_to_all(wannier_g, "rp", split_axis=3, concat_axis=1, tiled=True)
    right = moved.reshape(2 * moved.shape[1], -1)
    q_blocks = q_all.reshape(3, groups, block).transpose(1, 0, 2)

    def fourier_block(q_rows):
        left_real, left_imag = phases(q_rows, rp_coords)
        f_real = jnp.dot(left_real, right, preferred_element_type=jnp.float32).astype(jnp.bfloat16)
        f_imag = jnp.dot(left_imag, right, preferred_element_type=jnp.float32).astype(jnp.bfloat16)
        return jnp.stack([f_real, f_imag], 1)

    fourier = lax.map(fourier_block, q_blocks).reshape(total, 2, moved.shape[2], moved.shape[3])
    owned = one_exchange(fourier, ("rp", "pb"), ("rp", "pb"), (0, 0), (3, 2))
    select = (jnp.arange(k_vectors.shape[0]) == k_index[0]).astype(jnp.bfloat16)
    unit = jnp.einsum("k,kcnj->cnj", select, k_vectors, preferred_element_type=jnp.float32).astype(
        jnp.bfloat16
    )
    return rotate(owned, modes, unit, kq_vectors)


def solution(mesh):
    return jax.shard_map(
        local,
        mesh=mesh,
        in_specs=(
            P(None, "rp", "pb", None),
            P(),
            P(None, ("rp", "pb")),
            P(),
            P(),
            P(("rp", "pb"), None, None, None),
            P(("rp", "pb"), None, None, None),
        ),
        out_specs=P(("rp", "pb"), None, None, None),
        check_vma=False,
    )
```

profile of v0, /device:TPU:1, one launch (start us, length us, event | category | flops | bytes accessed | tf_op | source)
XLA Modules:
  0.0 424.2 jit_solution(9630580377085636037)
XLA Ops:
  0.0 3.0 copy.101
  3.0 6.2 %all-to-all-start = ((bf16[2,128,1,1152]{1,0,2,3:T(2,128)(2,1)}), bf16[2,128,1,1152]{1,0,2,3:T(2,128)(2,1)S(1)}, u32[]{:S(2)}, u32[]{:S(2)}) async-start(bf16[2,128,1,1152]{1,0,2,3:T(2,128)(2,1)} %copy.101), calls=%async_computation | async-start | bytes 1179648 | tf_op jit(solution)/shard_map/all_to_all | solution.py:67
  9.9 0.2 fusion.19
  10.3 350.8 %all-gather = s32[256,2,3]{2,1,0:T(2,128)S(1)} all-gather(s32[1,2,3]{2,1,0:T(2,128)S(1)} %bitcast.145), channel_id=1, replica_groups=mesh['rp'=8,'pb'=32] {'rp','pb'}, dimensions={0}, use_global_device_ids=true | all-gather | bytes 6168 | tf_op jit(solution)/shard_map/all_gather | solution.py:63
  361.4 0.5 copy.128
  362.0 27.2 %while.12 = (s32[]{:T(128)}, bf16[8,64,2,144]{3,2,1,0:T(2,128)(2,1)}, s32[8,3,64]{2,0,1:T(8,128)S(1)}, s32[3,1024]{1,0:T(4,128)S(1)}, bf16[2048,144]{1,0:T(8,128)(2,1)S(1)}, /*index=5*/s32[]{:T(128)}) while((s32[]{:T(128)}, bf16[8,64,2,144]{3,2,1,0:T(2,128)(2,1)}, s32[8,3,64]{2,0,1:T(8,128)S(1)}, s32[3,1024]{1,0:T(4,128)S(1)}, ...), condition=%wide.region_2.3_spmd, body=%wide.region_0.2_spmd.sunk | while | flops 78942208 | bytes 3112789 | solution.py:77
  362.1 0.9 cosine_convert_fusion.2
  363.1 1.0 fusion.51
  364.1 0.3 fusion.52
  364.4 0.3 fusion.53
  364.7 0.7 copy_dynamic-update-slice_fusion.2
  365.4 0.1 multiply_reduce_fusion.2
  365.5 0.9 cosine_convert_fusion.2
  366.5 1.0 fusion.51
  367.4 0.3 fusion.52
  367.7 0.3 fusion.53
  368.1 0.7 copy_dynamic-update-slice_fusion.2
  368.8 0.1 multiply_reduce_fusion.2
  368.9 0.9 cosine_convert_fusion.2
  369.9 1.0 fusion.51
  370.8 0.3 fusion.52
  371.1 0.3 fusion.53
  371.5 0.7 copy_dynamic-update-slice_fusion.2
  372.2 0.1 multiply_reduce_fusion.2
  372.3 0.9 cosine_convert_fusion.2
  373.3 1.0 fusion.51
  374.2 0.3 fusion.52
  374.5 0.3 fusion.53
  374.9 0.7 copy_dynamic-update-slice_fusion.2
  375.6 0.1 multiply_reduce_fusion.2
  375.7 0.9 cosine_convert_fusion.2
  376.6 1.0 fusion.51
  377.6 0.3 fusion.52
  377.9 0.3 fusion.53
  378.2 0.7 copy_dynamic-update-slice_fusion.2
  378.9 0.1 multiply_reduce_fusion.2
  379.1 0.9 cosine_convert_fusion.2
  380.0 1.0 fusion.51
  381.0 0.3 fusion.52
  381.3 0.3 fusion.53
  381.6 0.7 copy_dynamic-update-slice_fusion.2
  382.3 0.1 multiply_reduce_fusion.2
  382.5 0.9 cosine_convert_fusion.2
  383.4 1.0 fusion.51
  384.4 0.3 fusion.52
  384.7 0.3 fusion.53
  385.0 0.7 copy_dynamic-update-slice_fusion.2
  385.7 0.1 multiply_reduce_fusion.2
  385.9 0.9 cosine_convert_fusion.2
  386.8 1.0 fusion.51
  387.8 0.3 fusion.52
  388.1 0.3 fusion.53
  388.4 0.7 copy_dynamic-update-slice_fusion.2
  389.1 5.3 %all-to-all-start.1 = ((bf16[256,2,2,1,144]{4,2,1,3,0:T(2,128)(2,1)}), bf16[256,2,2,1,144]{4,2,1,3,0:T(2,128)(2,1)S(1)}, u32[]{:S(2)}, u32[]{:S(2)}) async-start(bf16[256,2,2,1,144]{4,2,1,3,0:T(2,128)(2,1)} %bitcast.38), calls=%async_computation.1 | async-start | bytes 1048576 | tf_op jit(solution)/shard_map/all_to_all | solution.py:28
  394.8 0.1 maximum_bitcast_fusion.1
  394.9 20.4 %all-to-all-done.1 = bf16[256,2,2,1,144]{4,2,1,3,0:T(2,128)(2,1)S(1)} async-done(((bf16[256,2,2,1,144]{4,2,1,3,0:T(2,128)(2,1)}), bf16[256,2,2,1,144]{4,2,1,3,0:T(2,128)(2,1)S(1)}, u32[]{:S(2)}, u32[]{:S(2)}) %all-to-all-start.1) | async-done | bytes 294944 | tf_op jit(solution)/shard_map/all_to_all | solution.py:28
  415.4 0.3 copy.109
  415.7 0.5 reshape.52
  416.2 2.8 reshape_reshape.3
  419.0 0.5 fusion.13
  419.5 0.5 fusion.14
  420.0 0.5 convolution_bitcast_fusion
  420.5 1.2 copy.114
  421.7 2.4 reshape.53
  (54 shorter events, 1.2 us)
Async XLA Ops:
  0.0 9.9 %copy-start = (bf16[8,2,32,32]{3,2,1,0:T(8,128)(2,1)S(1)}, bf16[8,2,32,32]{3,2,1,0:T(8,128)(2,1)}, u32[]{:S(2)}) copy-start(bf16[8,2,32,32]{3,2,1,0:T(8,128)(2,1)} %param.13) | copy-start | bytes 98308
  0.0 10.2 %copy-start.3 = (bf16[2,2,32,32]{3,2,1,0:T(8,128)(2,1)S(1)}, bf16[2,2,32,32]{3,2,1,0:T(8,128)(2,1)}, u32[]{:S(2)}) copy-start(bf16[2,2,32,32]{3,2,1,0:T(8,128)(2,1)} %param.14) | copy-start | bytes 24580
  0.0 10.3 %copy-start.4 = (s32[3,2]{0,1:T(2,128)S(1)}, s32[3,2]{0,1:T(2,128)}, u32[]{:S(2)}) copy-start(s32[3,2]{0,1:T(2,128)} %param.11) | copy-start | bytes 76
  0.0 361.3 %copy-start.2 = (bf16[2,2,36,36]{3,1,2,0:T(2,128)(2,1)S(1)}, bf16[2,2,36,36]{3,1,2,0:T(2,128)(2,1)}, u32[]{:S(2)}) copy-start(bf16[2,2,36,36]{3,1,2,0:T(2,128)(2,1)} %param.15) | copy-start | bytes 31108
  3.0 358.3 %all-to-all-start = ((bf16[2,128,1,1152]{1,0,2,3:T(2,128)(2,1)}), bf16[2,128,1,1152]{1,0,2,3:T(2,128)(2,1)S(1)}, u32[]{:S(2)}, u32[]{:S(2)}) async-start(bf16[2,128,1,1152]{1,0,2,3:T(2,128)(2,1)} %copy.101), calls=%async_computation | async-start | bytes 1179648 | tf_op jit(solution)/shard_map/all_to_all | solution.py:67
  9.2 352.8 %copy-start.1 = (s32[3,1024]{1,0:T(4,128)S(1)}, s32[3,1024]{1,0:T(4,128)}, u32[]{:S(2)}) copy-start(s32[3,1024]{1,0:T(4,128)} %param.10) | copy-start | bytes 36868
  389.1 26.2 %all-to-all-start.1 = ((bf16[256,2,2,1,144]{4,2,1,3,0:T(2,128)(2,1)}), bf16[256,2,2,1,144]{4,2,1,3,0:T(2,128)(2,1)S(1)}, u32[]{:S(2)}, u32[]{:S(2)}) async-start(bf16[256,2,2,1,144]{4,2,1,3,0:T(2,128)(2,1)} %bitcast.38), calls=%async_computation.1 | async-start | bytes 1048576 | tf_op jit(solution)/shard_map/all_to_all | solution.py:28
where the time goes:
time: 424 us
  blocking collectives  351 us (83%)
  waiting for transfers between devices  20.4 us (5%)
  local copies, waits for them, and re-layouts  17 us (4%)
  other arithmetic  16.8 us (4%)
  starting transfers between devices  11.5 us (3%)
  matrix products  6.36 us (2%)
    all_gather x1, blocking collectives, local(): q_all = lax.all_gather(q_coords, ('rp', 'pb'), axis=1, tiled=True)  351 us
    all_to_all x1, waiting for transfers between devices, one_exchange(): parts = lax.all_to_all(parts, axis, split_axis=0, concat_axis=0, tiled=True)  20.4 us
  transfers between devices with their start and end apart: 2, of which 1 were waited for; matrix products, arithmetic and copies ran while one was open for 0% of the time, Pallas kernels for 0%

commit v1 on v0

--- a/solution.py
+++ b/solution.py
@@ -60,7 +60,7 @@
 
 
 def local(wannier_g, rp_coords, q_coords, k_index, k_vectors, kq_vectors, modes):
-    q_all = lax.all_gather(q_coords, ("rp", "pb"), axis=1, tiled=True)
+    q_all = jnp.concatenate(lax.all_gather(q_coords, ("rp", "pb")), axis=1)
     total = q_all.shape[1]
     groups = lax.axis_size("rp")
     block = total // groups

time: 424 us -> 424 us (level)
  no operation moved by 1% of the time
where the time goes in v1:
time: 424 us
  blocking collectives  351 us (83%)
  waiting for transfers between devices  20.4 us (5%)
  local copies, waits for them, and re-layouts  16.9 us (4%)
  other arithmetic  16.8 us (4%)
  starting transfers between devices  11.5 us (3%)
  matrix products  6.36 us (2%)
    all_gather x1, blocking collectives, local(): q_all = jnp.concatenate(lax.all_gather(q_coords, ('rp', 'pb')), axis=1)  351 us
    all_to_all x1, waiting for transfers between devices, one_exchange(): parts = lax.all_to_all(parts, axis, split_axis=0, concat_axis=0, tiled=True)  20.4 us
  transfers between devices with their start and end apart: 2, of which 1 were waited for; matrix products, arithmetic and copies ran while one was open for 0% of the time, Pallas kernels for 0%

profile of v1, /device:TPU:1, one launch (start us, length us, event | category | flops | bytes accessed | tf_op | source)
XLA Modules:
  0.0 424.0 jit_solution(14274803977324020886)
XLA Ops:
  0.0 3.0 copy.98
  3.0 6.2 %all-to-all-start = ((bf16[2,128,1,1152]{1,0,2,3:T(2,128)(2,1)}), bf16[2,128,1,1152]{1,0,2,3:T(2,128)(2,1)S(1)}, u32[]{:S(2)}, u32[]{:S(2)}) async-start(bf16[2,128,1,1152]{1,0,2,3:T(2,128)(2,1)} %copy.98), calls=%async_computation | async-start | bytes 1179648 | tf_op jit(solution)/shard_map/all_to_all | solution.py:67
  9.9 0.2 fusion.19
  10.3 350.8 %all-gather.1 = s32[256,3,2]{1,2,0:T(2,128)S(1)} all-gather(s32[1,3,2]{1,2,0:T(2,128)S(1)} %bitcast.141), channel_id=2, replica_groups=mesh['rp'=8,'pb'=32] {'rp','pb'}, dimensions={0}, use_global_device_ids=true | all-gather | bytes 6168 | tf_op jit(solution)/shard_map/all_gather | solution.py:63
  361.1 0.1 copy.97
  361.4 0.5 copy.124
  361.9 27.1 %while.12 = (s32[]{:T(128)}, bf16[8,64,2,144]{3,2,1,0:T(2,128)(2,1)}, s32[8,3,64]{2,1,0:T(4,128)S(1)}, s32[3,1024]{1,0:T(4,128)S(1)}, bf16[2048,144]{1,0:T(8,128)(2,1)S(1)}, /*index=5*/s32[]{:T(128)}) while((s32[]{:T(128)}, bf16[8,64,2,144]{3,2,1,0:T(2,128)(2,1)}, s32[8,3,64]{2,1,0:T(4,128)S(1)}, s32[3,1024]{1,0:T(4,128)S(1)}, ...), condition=%wide.region_2.3_spmd, body=%wide.region_0.2_spmd.sunk | while | flops 78942208 | bytes 3111253 | solution.py:77
  362.1 0.9 cosine_convert_fusion.2
  363.0 1.0 fusion.51
  364.0 0.3 fusion.52
  364.3 0.3 fusion.53
  364.6 0.7 copy_dynamic-update-slice_fusion.2
  365.3 0.1 multiply_reduce_fusion.2
  365.4 0.9 cosine_convert_fusion.2
  366.4 1.0 fusion.51
  367.4 0.3 fusion.52
  367.7 0.3 fusion.53
  368.0 0.7 copy_dynamic-update-slice_fusion.2
  368.7 0.1 multiply_reduce_fusion.2
  368.8 0.9 cosine_convert_fusion.2
  369.8 1.0 fusion.51
  370.8 0.3 fusion.52
  371.1 0.3 fusion.53
  371.4 0.7 copy_dynamic-update-slice_fusion.2
  372.1 0.1 multiply_reduce_fusion.2
  372.2 0.9 cosine_convert_fusion.2
  373.2 1.0 fusion.51
  374.1 0.3 fusion.52
  374.4 0.3 fusion.53
  374.8 0.7 copy_dynamic-update-slice_fusion.2
  375.5 0.1 multiply_reduce_fusion.2
  375.6 0.9 cosine_convert_fusion.2
  376.5 1.0 fusion.51
  377.5 0.3 fusion.52
  377.8 0.3 fusion.53
  378.1 0.7 copy_dynamic-update-slice_fusion.2
  379.0 0.9 cosine_convert_fusion.2
  379.9 1.0 fusion.51
  380.9 0.3 fusion.52
  381.2 0.3 fusion.53
  381.5 0.7 copy_dynamic-update-slice_fusion.2
  382.2 0.1 multiply_reduce_fusion.2
  382.4 0.9 cosine_convert_fusion.2
  383.3 1.0 fusion.51
  384.3 0.3 fusion.52
  384.6 0.3 fusion.53
  384.9 0.7 copy_dynamic-update-slice_fusion.2
  385.6 0.1 multiply_reduce_fusion.2
  385.7 0.9 cosine_convert_fusion.2
  386.7 1.0 fusion.51
  387.7 0.3 fusion.52
  388.0 0.3 fusion.53
  388.3 0.7 copy_dynamic-update-slice_fusion.2
  389.0 5.3 %all-to-all-start.1 = ((bf16[256,2,2,1,144]{4,2,1,3,0:T(2,128)(2,1)}), bf16[256,2,2,1,144]{4,2,1,3,0:T(2,128)(2,1)S(1)}, u32[]{:S(2)}, u32[]{:S(2)}) async-start(bf16[256,2,2,1,144]{4,2,1,3,0:T(2,128)(2,1)} %bitcast.37), calls=%async_computation.1 | async-start | bytes 1048576 | tf_op jit(solution)/shard_map/all_to_all | solution.py:28
  394.6 0.1 maximum_bitcast_fusion.1
  394.8 20.4 %all-to-all-done.1 = bf16[256,2,2,1,144]{4,2,1,3,0:T(2,128)(2,1)S(1)} async-done(((bf16[256,2,2,1,144]{4,2,1,3,0:T(2,128)(2,1)}), bf16[256,2,2,1,144]{4,2,1,3,0:T(2,128)(2,1)S(1)}, u32[]{:S(2)}, u32[]{:S(2)}) %all-to-all-start.1) | async-done | bytes 294944 | tf_op jit(solution)/shard_map/all_to_all | solution.py:28
  415.3 0.3 copy.105
  415.6 0.5 reshape.52
  416.1 2.8 reshape_reshape.7
  418.9 0.5 fusion.13
  419.4 0.5 fusion.14
  419.8 0.5 convolution_bitcast_fusion
  420.4 1.2 copy.110
  421.6 2.4 reshape.53
  (45 shorter events, 1.1 us)
Async XLA Ops:
  0.0 9.9 %copy-start = (bf16[8,2,32,32]{3,2,1,0:T(8,128)(2,1)S(1)}, bf16[8,2,32,32]{3,2,1,0:T(8,128)(2,1)}, u32[]{:S(2)}) copy-start(bf16[8,2,32,32]{3,2,1,0:T(8,128)(2,1)} %param.13) | copy-start | bytes 98308
  0.0 10.2 %copy-start.3 = (bf16[2,2,32,32]{3,2,1,0:T(8,128)(2,1)S(1)}, bf16[2,2,32,32]{3,2,1,0:T(8,128)(2,1)}, u32[]{:S(2)}) copy-start(bf16[2,2,32,32]{3,2,1,0:T(8,128)(2,1)} %param.14) | copy-start | bytes 24580
  0.0 10.3 %copy-start.4 = (s32[3,2]{0,1:T(2,128)S(1)}, s32[3,2]{0,1:T(2,128)}, u32[]{:S(2)}) copy-start(s32[3,2]{0,1:T(2,128)} %param.11) | copy-start | bytes 76
  0.0 361.2 %copy-start.2 = (bf16[2,2,36,36]{3,1,2,0:T(2,128)(2,1)S(1)}, bf16[2,2,36,36]{3,1,2,0:T(2,128)(2,1)}, u32[]{:S(2)}) copy-start(bf16[2,2,36,36]{3,1,2,0:T(2,128)(2,1)} %param.15) | copy-start | bytes 31108
  3.0 358.3 %all-to-all-start = ((bf16[2,128,1,1152]{1,0,2,3:T(2,128)(2,1)}), bf16[2,128,1,1152]{1,0,2,3:T(2,128)(2,1)S(1)}, u32[]{:S(2)}, u32[]{:S(2)}) async-start(bf16[2,128,1,1152]{1,0,2,3:T(2,128)(2,1)} %copy.98), calls=%async_computation | async-start | bytes 1179648 | tf_op jit(solution)/shard_map/all_to_all | solution.py:67
  9.2 352.7 %copy-start.1 = (s32[3,1024]{1,0:T(4,128)S(1)}, s32[3,1024]{1,0:T(4,128)}, u32[]{:S(2)}) copy-start(s32[3,1024]{1,0:T(4,128)} %param.10) | copy-start | bytes 36868
  389.0 26.2 %all-to-all-start.1 = ((bf16[256,2,2,1,144]{4,2,1,3,0:T(2,128)(2,1)}), bf16[256,2,2,1,144]{4,2,1,3,0:T(2,128)(2,1)S(1)}, u32[]{:S(2)}, u32[]{:S(2)}) async-start(bf16[256,2,2,1,144]{4,2,1,3,0:T(2,128)(2,1)} %bitcast.37), calls=%async_computation.1 | async-start | bytes 1048576 | tf_op jit(solution)/shard_map/all_to_all | solution.py:28
